TPU v7x, 512 devices: a whole 4x4x16 slice. The times are simulated.
512 devices in a mesh: row: 64 (over y_hi, z, core), head: 8 (over x, y_lo).
Axes of the slice: x: 4, y: 4 (y_hi: 2, y_lo: 2; y = y_hi * 2 + y_lo), z: 16, core: 2. Of those that a mesh axis runs over, the one named last changes fastest.
Arguments:
- pair_input: bfloat16 [512, 512, 128], P(('row', 'head')), may hold values from -6 to 6
- cotangent: bfloat16 [512, 512, 128], P(('row', 'head')), may hold values from -24 to 24
- residue_mask: int32 [512], replicated, may hold values from 0 to 1, as said below
- norm_gain: float32 [2, 128], replicated, may hold values from 0.5 to 1.5
- norm_shift: float32 [2, 128], replicated, may hold values from -3 to 3
- proj_weights: bfloat16 [2, 4, 128, 128], replicated, may hold values from -0.5 to 0.5
- gate_bias: float32 [2, 128], replicated, may hold values from -4 to 4
- out_weights: bfloat16 [2, 128, 128], replicated, may hold values from -1.0546875 to 1.0546875
- bias_weights: bfloat16 [2, 128, 4], replicated, may hold values from -1.06066017 to 1.06066017
Outputs:
- pair_grad: float32 [512, 512, 128], P(('row', 'head'))
- proj_grad: float32 [2, 4, 128, 128], replicated
- gate_bias_grad: float32 [2, 128], replicated
- out_grad: float32 [2, 128, 128], replicated
- bias_weight_grad: float32 [2, 128, 4], replicated
- gain_grad: float32 [2, 128], replicated
- shift_grad: float32 [2, 128], replicated
Inputs may be any that keep to these rules, and one draw needn't show every extreme that they name: `residue_mask`: 1 for the first residues of the crop and 0 for the padding after them; at least half of the 512 residues are 1.
All inputs are finite; a program needn't handle non-finite values.
Results may differ from a plain program's by a relative error of at most 0.02.
The roundings to bfloat16 on the way count: a program that leaves them out, or rounds other values in their place, can miss the bound.
Values may be sent and summed in bfloat16 or wider, within the bound.
No kernel may reach another device: no remote copies, remote signals or barrier semaphores. Data moves between devices by JAX's collectives and lax.ppermute only.
A program may use at most 64 MiB of HBM per device.

v0:
```python
import math
import jax
import jax.numpy as jnp
from jax import lax
from jax.sharding import Mesh
from jax.sharding import PartitionSpec as P

HEAD = ("head_0", "head_1")
ROW_HEAD = ("row", "head_0", "head_1")
EPS = 1e-05
MASKED = 1000000000.0


def whole_of(x, axes, dim):
    for axis in reversed(axes):
        x = lax.all_gather(x, axis, axis=dim, tiled=True)
    return x


def joined_along(parts, dim):
    parts = jnp.moveaxis(parts, 0, dim)
    dims = parts.shape
    return parts.reshape(*dims[:dim], dims[dim] * dims[dim + 1], *dims[dim + 2 :])


def from_everyone(x, axis):
    length = lax.axis_size(axis)
    return lax.all_to_all(jnp.broadcast_to(x[None], (length, *x.shape)), axis, 0, 0, tiled=True)


def gather_directly(x, axis, dim):
    return joined_along(from_everyone(x, axis), dim)


def split_up(x, dim, length):
    dims = x.shape
    parts = x.reshape(*dims[:dim], length, dims[dim] // length, *dims[dim + 1 :])
    return jnp.moveaxis(parts, dim, 0)


def sent_and_summed(x, axis, dim):
    length = lax.axis_size(axis)
    parts = lax.all_to_all(split_up(x, dim, length), axis, 0, 0, tiled=True)
    return jnp.sum(parts.astype(jnp.float32), axis=0)


def summed_on_arrival(x, axis, dim):
    parts = split_up(x, dim, lax.axis_size(axis))
    arrived = lax.all_to_all(parts, axis, split_axis=0, concat_axis=0, tiled=True)
    return arrived.sum(axis=0)


def joined_exchange(x, axis, axes, splits, concats):
    sizes = [lax.axis_size(a) for a in axes]
    parts = split_up(x, splits[0], sizes[0])
    parts = jnp.moveaxis(split_up(parts, splits[1] + 1, sizes[1]), 0, 1)
    inside = parts.shape[2:]
    parts = parts.reshape(-1, *inside)
    parts = lax.all_to_all(parts, axis, split_axis=0, concat_axis=0, tiled=True)
    parts = joined_along(parts.reshape(*sizes, *inside), concats[0] + 1)
    return joined_along(parts, concats[1])


def layer_norm(values, norm_scale, norm_offset):
    floats = values.astype(jnp.float32)
    centred = floats - jnp.mean(floats, axis=-1, keepdims=True)
    inverse = lax.rsqrt(jnp.mean(centred * centred, axis=-1, keepdims=True) + EPS)
    normed = centred * inverse
    return (normed, inverse, (normed * norm_scale + norm_offset).astype(jnp.bfloat16))


def norm_backward(grad_normal, normed, inverse, norm_scale):
    grad_hat = grad_normal * norm_scale
    first_mean = jnp.mean(grad_hat, axis=-1, keepdims=True)
    second_mean = jnp.mean(grad_hat * normed, axis=-1, keepdims=True)
    return inverse * (grad_hat - first_mean - normed * second_mean)


def class_columns(values, head_index, row_count, head_count, slab_rows):
    leading = values.shape[0]
    shaped = values.reshape(leading, row_count, head_count, slab_rows, values.shape[-1])
    picked = lax.dynamic_index_in_dim(shaped, head_index, axis=2, keepdims=False)
    return picked.reshape(leading, row_count * slab_rows, values.shape[-1])


def forward_block(pair_rows, key_bias, params, layout):
    norm_scale, norm_offset, projection, gate_offset, out_proj, bias_proj = params
    slab_rows, row_count, head_count, head_index = layout
    head_total = bias_proj.shape[1]
    inner_width = projection.shape[2]
    head_size = inner_width // head_total
    query_scale = 1.0 / math.sqrt(head_size)
    normed, inverse, normal_own = layer_norm(pair_rows, norm_scale, norm_offset)
    normal_rows = whole_of(normal_own, HEAD, 0)
    bias_own = jnp.einsum(
        "snc,ch->hsn", normal_own, bias_proj, preferred_element_type=jnp.float32
    ).astype(jnp.bfloat16)
    bias_query = gather_directly(bias_own, "row", 1)
    normal_query = class_columns(normal_rows, head_index, row_count, head_count, slab_rows)
    block_rows = normal_query.shape[0]
    query_count = normal_query.shape[1]
    key_count = normal_rows.shape[1]
    queries = (
        jnp.dot(normal_query, projection[0], preferred_element_type=jnp.float32) * query_scale
    ).astype(jnp.bfloat16)
    joined_weights = jnp.concatenate([projection[1], projection[2]], axis=1)
    key_value = jnp.dot(normal_rows, joined_weights, preferred_element_type=jnp.float32).astype(
        jnp.bfloat16
    )
    gate_values = jax.nn.sigmoid(
        jnp.dot(normal_query, projection[3], preferred_element_type=jnp.float32) + gate_offset
    )
    head_queries = queries.reshape(block_rows, query_count, head_total, head_size).transpose(
        2, 0, 1, 3
    )
    head_pairs = key_value.reshape(block_rows, key_count, 2, head_total, head_size).transpose(
        2, 3, 0, 1, 4
    )

    def attend(inputs):
        query_head, key_head, value_head, bias_head = inputs
        logits = jnp.einsum(
            "rqd,rnd->rqn", query_head, key_head, preferred_element_type=jnp.float32
        )
        logits = logits + bias_head.astype(jnp.float32)[None] + key_bias
        largest = jnp.max(logits, axis=-1, keepdims=True)
        weights = jnp.exp(logits - largest)
        total = jnp.sum(weights, axis=-1, keepdims=True)
        soft_weights = weights / total
        attended = jnp.einsum(
            "rqn,rnd->rqd",
            soft_weights.astype(jnp.bfloat16),
            value_head,
            preferred_element_type=jnp.float32,
        )
        return ((largest + jnp.log(total))[..., 0], attended)

    log_totals, attended = lax.map(attend, (head_queries, head_pairs[0], head_pairs[1], bias_query))
    attended = attended.transpose(1, 2, 0, 3).reshape(block_rows, query_count, inner_width)
    gated_out = (gate_values * attended).astype(jnp.bfloat16)
    update = jnp.dot(gated_out, out_proj, preferred_element_type=jnp.float32).astype(jnp.bfloat16)
    saved_state = (
        normed,
        inverse,
        normal_own,
        normal_rows,
        normal_query,
        head_queries,
        head_pairs,
        bias_query,
        gate_values,
        attended,
        gated_out,
        log_totals,
    )
    return (saved_state, update)


def backward_block(saved_state, grad_query, key_bias, params, layout):
    norm_scale, norm_offset, projection, gate_offset, out_proj, bias_proj = params
    slab_rows, row_count, head_count, head_index = layout
    (
        normed,
        inverse,
        normal_own,
        normal_rows,
        normal_query,
        head_queries,
        head_pairs,
        bias_query,
        gate_values,
        attended,
        gated_out,
        log_totals,
    ) = saved_state
    channels = normal_own.shape[2]
    head_total, block_rows, query_count, head_size = head_queries.shape
    key_count = normal_rows.shape[1]
    inner_width = head_total * head_size
    query_scale = 1.0 / math.sqrt(head_size)
    grad_gated = jnp.dot(grad_query, out_proj.T, preferred_element_type=jnp.float32)
    grad_att = (grad_gated * gate_values).astype(jnp.bfloat16)
    grad_pre = (grad_gated * attended * gate_values * (1.0 - gate_values)).astype(jnp.bfloat16)
    head_grads = grad_att.reshape(block_rows, query_count, head_total, head_size).transpose(
        2, 0, 1, 3
    )

    def differentiate(inputs):
        total_head, query_head, key_head, value_head, bias_head, grad_head = inputs
        logits = jnp.einsum(
            "rqd,rnd->rqn", query_head, key_head, preferred_element_type=jnp.float32
        )
        logits = logits + bias_head.astype(jnp.float32)[None] + key_bias
        soft_weights = jnp.exp(logits - total_head[..., None])
        grad_weights = jnp.einsum(
            "rqd,rnd->rqn", grad_head, value_head, preferred_element_type=jnp.float32
        )
        grad_logits = soft_weights * (
            grad_weights - jnp.sum(soft_weights * grad_weights, axis=-1, keepdims=True)
        )
        logits_half = grad_logits.astype(jnp.bfloat16)
        grad_queries = (
            jnp.einsum("rqn,rnd->rqd", logits_half, key_head, preferred_element_type=jnp.float32)
            * query_scale
        ).astype(jnp.bfloat16)
        grad_keys = jnp.einsum(
            "rqn,rqd->rnd", logits_half, query_head, preferred_element_type=jnp.float32
        ).astype(jnp.bfloat16)
        grad_values = jnp.einsum(
            "rqn,rqd->rnd",
            soft_weights.astype(jnp.bfloat16),
            grad_head,
            preferred_element_type=jnp.float32,
        ).astype(jnp.bfloat16)
        return (grad_queries, grad_keys, grad_values, jnp.sum(grad_logits, axis=0))

    grad_queries, grad_keys, grad_values, grad_bias = lax.map(
        differentiate,
        (log_totals, head_queries, head_pairs[0], head_pairs[1], bias_query, head_grads),
    )
    grad_queries = grad_queries.transpose(1, 2, 0, 3).reshape(block_rows, query_count, inner_width)
    key_weights = projection[1].reshape(channels, head_total, head_size).transpose(1, 2, 0)
    value_weights = projection[2].reshape(channels, head_total, head_size).transpose(1, 2, 0)
    query_side = jnp.dot(grad_queries, projection[0].T, preferred_element_type=jnp.float32)
    query_side = query_side + jnp.dot(grad_pre, projection[3].T, preferred_element_type=jnp.float32)
    count = slab_rows * lax.axis_size(HEAD)
    term = jnp.einsum("hrnd,hdc->rnc", grad_keys, key_weights, preferred_element_type=jnp.float32)
    term = term + jnp.einsum(
        "hrnd,hdc->rnc", grad_values, value_weights, preferred_element_type=jnp.float32
    )
    shaped = term.reshape(count, row_count, head_count, slab_rows, channels)
    current = lax.dynamic_slice_in_dim(shaped, head_index, 1, 2)
    query_slice = query_side.reshape(count, row_count, 1, slab_rows, channels)
    shaped = lax.dynamic_update_slice_in_dim(shaped, current + query_slice, head_index, 2)
    grad_normal = sent_and_summed(
        shaped.reshape(count, key_count, channels).astype(jnp.bfloat16), HEAD, 0
    )
    bias_total = summed_on_arrival(grad_bias, "row", 1)
    bias_half = bias_total.astype(jnp.bfloat16)
    grad_normal = grad_normal + jnp.einsum(
        "hsn,ch->snc", bias_half, bias_proj, preferred_element_type=jnp.float32
    )
    grad_pair = norm_backward(grad_normal, normed, inverse, norm_scale)
    projection_grads = jnp.stack(
        [
            jnp.einsum(
                "rqc,rqe->ce", normal_query, grad_queries, preferred_element_type=jnp.float32
            ),
            jnp.einsum(
                "rnc,hrnd->chd", normal_rows, grad_keys, preferred_element_type=jnp.float32
            ).reshape(channels, inner_width),
            jnp.einsum(
                "rnc,hrnd->chd", normal_rows, grad_values, preferred_element_type=jnp.float32
            ).reshape(channels, inner_width),
            jnp.einsum("rqc,rqe->ce", normal_query, grad_pre, preferred_element_type=jnp.float32),
        ]
    )
    weight_grads = (
        projection_grads,
        jnp.sum(grad_pre.astype(jnp.float32), axis=(0, 1)),
        jnp.einsum("rqe,rqc->ec", gated_out, grad_query, preferred_element_type=jnp.float32),
        jnp.einsum("snc,hsn->ch", normal_own, bias_half, preferred_element_type=jnp.float32),
        jnp.sum(grad_normal * normed, axis=(0, 1)),
        jnp.sum(grad_normal, axis=(0, 1)),
    )
    return (grad_pair, weight_grads)


def to_queries(grad_rows, layout):
    slab_rows, row_count, head_count, head_index = layout
    channels = grad_rows.shape[2]
    shaped = grad_rows.reshape(slab_rows, row_count, head_count, slab_rows, channels)
    moved = lax.all_to_all(shaped, HEAD, split_axis=2, concat_axis=0, tiled=True)
    return moved.reshape(slab_rows * head_count, row_count * slab_rows, channels)


def local(
    pair_input,
    cotangent,
    residue_mask,
    norm_gain,
    norm_shift,
    proj_weights,
    gate_bias,
    out_weights,
    bias_weights,
):
    slab_rows = pair_input.shape[0]
    channels = pair_input.shape[2]
    row_count = lax.axis_size("row")
    head_count = lax.axis_size(HEAD)
    layout = (slab_rows, row_count, head_count, lax.axis_index(HEAD))
    key_bias = (residue_mask.astype(jnp.float32) - 1.0) * MASKED
    params = [
        (
            norm_gain[which],
            norm_shift[which],
            proj_weights[which],
            gate_bias[which],
            out_weights[which],
            bias_weights[which],
        )
        for which in range(2)
    ]
    first_state, first_update = forward_block(pair_input, key_bias, params[0], layout)
    returned = lax.all_to_all(
        first_update.reshape(slab_rows * head_count, row_count, 1, slab_rows, channels),
        HEAD,
        split_axis=0,
        concat_axis=2,
        tiled=True,
    )
    after_first = (
        pair_input.astype(jnp.float32)
        + returned.reshape(slab_rows, -1, channels).astype(jnp.float32)
    ).astype(jnp.bfloat16)
    joined = jnp.concatenate([after_first, cotangent], axis=2)
    moved = joined_exchange(
        joined.reshape(1, 1, slab_rows, row_count, head_count, slab_rows, 2 * channels),
        ROW_HEAD,
        ("row", HEAD),
        (3, 4),
        (0, 1),
    )
    flipped = moved.reshape(-1, slab_rows, 2 * channels).transpose(1, 0, 2)
    second_state, second_update = forward_block(
        flipped[:, :, :channels], key_bias, params[1], layout
    )
    second_grad, second_weights = backward_block(
        second_state, to_queries(flipped[:, :, channels:], layout), key_bias, params[1], layout
    )
    sent_back = joined_exchange(
        second_grad.astype(jnp.bfloat16).reshape(
            1, 1, slab_rows, row_count, head_count, slab_rows, channels
        ),
        ROW_HEAD,
        ("row", HEAD),
        (3, 4),
        (0, 1),
    )
    end_grad = sent_back.reshape(-1, slab_rows, channels).transpose(1, 0, 2)
    grad_after = cotangent.astype(jnp.float32) + end_grad.astype(jnp.float32)
    start_grad, first_weights = backward_block(
        first_state,
        to_queries(grad_after.astype(jnp.bfloat16), layout),
        key_bias,
        params[0],
        layout,
    )
    pair_grad = grad_after + start_grad
    combined = [
        jnp.stack([start_part, end_part])
        for start_part, end_part in zip(first_weights, second_weights)
    ]
    stacked = lax.psum(
        (combined[0], combined[1], combined[2], combined[3], combined[4], combined[5]), ROW_HEAD
    )
    return (pair_grad, stacked[0], stacked[1], stacked[2], stacked[3], stacked[4], stacked[5])


def solution(mesh):
    finer = Mesh(mesh.devices.reshape(mesh.shape["row"], 4, 2), ("row", "head_0", "head_1"))
    in_specs = (P(ROW_HEAD, None, None), P(ROW_HEAD, None, None), P(), P(), P(), P(), P(), P(), P())
    out_specs = (P(ROW_HEAD, None, None), P(), P(), P(), P(), P(), P())
    return jax.shard_map(local, mesh=finer, in_specs=in_specs, out_specs=out_specs, check_vma=False)
```

profile of v0, /device:TPU:1, one launch (start us, length us, event | category | flops | bytes accessed | tf_op | source)
XLA Modules:
  0.0 951.6 jit_solution(1266465462356417426)
XLA Ops:
  11.9 5.2 all_gather.12
  18.7 20.5 %all-to-all-start = ((bf16[64,4,1,512]{3,1,2,0:T(4,128)(2,1)}), bf16[64,4,1,512]{3,1,2,0:T(4,128)(2,1)S(1)}, u32[]{:S(2)}, u32[]{:S(2)}) async-start(bf16[64,4,1,512]{3,1,2,0:T(4,128)(2,1)} %broadcast_in_dim.57), calls=%async_computation | async-start | bytes 524288 | tf_op jit(solution)/shard_map/all_to_all | solution.py:28
  40.8 22.2 %all-to-all-done = bf16[64,4,1,512]{3,1,2,0:T(4,128)(2,1)S(1)} async-done(((bf16[64,4,1,512]{3,1,2,0:T(4,128)(2,1)}), bf16[64,4,1,512]{3,1,2,0:T(4,128)(2,1)S(1)}, u32[]{:S(2)}, u32[]{:S(2)}) %all-to-all-start) | async-done | bytes 262176 | tf_op jit(solution)/shard_map/all_to_all | solution.py:28
  63.1 1.6 constant_dynamic-slice_fusion.3
  68.0 11.2 %while.56 = (s32[]{:T(128)}, f32[4,8,64]{2,1,0:T(8,128)}, f32[4,8,64,32]{2,3,1,0:T(8,128)S(1)}, bf16[4,8,64,32]{2,3,1,0:T(8,128)(2,1)S(1)}, bf16[4,8,512,32]{2,3...) while((s32[]{:T(128)}, f32[4,8,64]{2,1,0:T(8,128)}, ...), condition=%wide.region_5.6_spmd, body=%wide.region_2.5_spmd.sunk | while | flops 35683840 | bytes 4221537 | solution.py:138
  81.3 9.2 all_to_all.79
  92.2 36.4 %all_to_all.80 = bf16[512,2,128]{2,1,0:T(2,128)(2,1)S(1)} all-to-all(bf16[512,2,128]{2,1,0:T(2,128)(2,1)S(1)} %reshape.464), channel_id=1, replica_groups=mesh['row'=64,'head_0'=4,'head_1'=2] {'row','head_0','head_1'}, dimensions={0} | all-to-all | bytes 524288 | tf_op jit(solution)/shard_map/all_to_all | solution.py:59
  129.4 6.0 all_gather.14
  136.1 3.4 all-to-all-start.4
  139.6 5.0 all-to-all-done.4
  145.4 6.2 all-to-all-start.3
  152.1 23.3 %all-to-all-done.3 = bf16[64,4,1,512]{3,1,2,0:T(4,128)(2,1)S(1)} async-done(((bf16[64,4,1,512]{3,1,2,0:T(4,128)(2,1)}), bf16[64,4,1,512]{3,1,2,0:T(4,128)(2,1)S(1)}, u32[]{:S(2)}, u32[]{:S(2)}) %all-to-all-start.3) | async-done | bytes 262176 | tf_op jit(solution)/shard_map/all_to_all | solution.py:28
  176.1 1.9 convolution_convert_fusion.4
  178.3 1.6 slice_bitcast_fusion
  182.5 18.3 %while.57 = (s32[]{:T(128)}, f32[4,8,64]{2,1,0:T(8,128)}, f32[4,8,64,32]{2,3,1,0:T(8,128)S(1)}, bf16[4,8,64,32]{2,3,1,0:T(8,128)(2,1)S(1)}, bf16[4,8,512,32]{2,3...) while((s32[]{:T(128)}, f32[4,8,64]{2,1,0:T(8,128)}, ...), condition=%wide.region_11.12_spmd, body=%wide.region_8.11_spmd.sunk | while | flops 35683840 | bytes 4221537 | solution.py:138
  207.3 51.8 %while.58 = (s32[]{:T(128)}, bf16[4,8,64,32]{2,3,1,0:T(8,128)(2,1)}, bf16[4,8,512,32]{2,3,1,0:T(8,128)(2,1)}, bf16[4,8,512,32]{2,3,1,0:T(8,128)(2,1)}, f32[4,64,...) while((s32[]{:T(128)}, ...), condition=%wide.region_15.16_spmd, body=%wide.region_12.15_spmd.sunk | while | flops 86801920 | bytes 10505361 | solution.py:217
  213.0 3.6 dynamic_update_slice.78
  216.6 1.8 fusion.300
  218.4 1.8 fusion.298
  225.9 3.6 dynamic_update_slice.78
  229.6 1.8 fusion.300
  231.4 1.8 fusion.298
  238.9 3.6 dynamic_update_slice.78
  242.5 1.8 fusion.300
  244.3 1.8 fusion.298
  251.8 3.6 dynamic_update_slice.78
  255.5 1.8 fusion.300
  257.2 1.8 fusion.298
  259.1 1.8 fusion.204
  262.9 1.7 fusion.100
  264.6 6.1 dynamic_update_slice.47
  270.9 18.0 %all_to_all.81 = bf16[8,1,512,128]{3,2,1,0:T(8,128)(2,1)S(1)} all-to-all(bf16[8,1,512,128]{3,2,1,0:T(8,128)(2,1)S(1)} %convert_bitcast_fusion.1), channel_id=1, replica_groups=mesh['row'=64,'head_0'=4,'head_1'=2] {'head_0','head_1'}, dimensions={0} | all-to-all | bytes 2097152 | tf_op jit(solution)/shard_map/all_to_all | solution.py:43
  288.8 4.7 all-to-all-start.6
  294.4 32.6 %all-to-all-done.6 = f32[64,4,1,512]{3,1,2,0:T(4,128)S(1)} async-done(((f32[64,4,1,512]{3,1,2,0:T(4,128)}), f32[64,4,1,512]{3,1,2,0:T(4,128)S(1)}, u32[]{:S(2)}, u32[]{:S(2)}) %all-to-all-start.6) | async-done | bytes 524320 | tf_op jit(solution)/shard_map/all_to_all | solution.py:49
  327.1 1.9 fusion.141
  331.6 9.3 all-to-all-start.7
  340.9 24.7 %all-to-all-done.7 = bf16[512,1,1,1,1,1,1,128]{7,6,5,4,3,2,1,0:T(2,128)(2,1)S(1)} async-done(((bf16[512,1,1,1,1,1,1,128]{7,6,5,4,3,2,1,0:T(2,128)(2,1)}), bf16[512,1,1,1,1,1,1,128]{7,6,5,4,3,2,1,0:T(2,128)(2,1)S(1)}, u32[]{:S(2)}, u32[]{:S(2)}) %all-to-all-start.7) | async-done | bytes 131104 | tf_op jit(solution)/shard_map/all_to_all | solution.py:59
  367.2 3.4 all-to-all-start.8
  370.6 1.6 fusion.109
  373.0 2.8 all-to-all-done.8
  381.1 40.7 %while.59 = (s32[]{:T(128)}, bf16[4,8,64,32]{2,3,1,0:T(8,128)(2,1)}, bf16[4,8,512,32]{2,3,1,0:T(8,128)(2,1)}, bf16[4,8,512,32]{2,3,1,0:T(8,128)(2,1)}, f32[4,64,...) while((s32[]{:T(128)}, ...), condition=%wide.region_23.24_spmd, body=%wide.region_20.23_spmd.sunk | while | flops 86801920 | bytes 10505361 | solution.py:217
  385.8 3.6 dynamic_update_slice.82
  396.0 3.6 dynamic_update_slice.82
  406.1 3.6 dynamic_update_slice.82
  416.3 3.6 dynamic_update_slice.82
  421.8 1.8 fusion.205
  425.6 1.7 fusion.101
  427.3 6.1 dynamic_update_slice.48
  434.5 3.7 all-to-all-start.9
  438.2 2.3 fusion.107
  440.5 1.7 copy.188
  442.1 1.8 convolution_bitcast_fusion.4
  444.0 1.8 convolution_bitcast_fusion.6
  445.8 2.0 convolution_bitcast_fusion.2
  447.7 5.1 all-to-all-done.9
  452.8 6.7 all-to-all-start.10
  459.6 1.7 maximum_bitcast_fusion.2
  461.4 2.3 fusion.113
  463.7 1.6 copy.184
  465.3 1.7 fusion.111
  470.6 22.2 %all-to-all-done.10 = f32[64,4,1,512]{3,1,2,0:T(4,128)} async-done(((f32[64,4,1,512]{3,1,2,0:T(4,128)}), f32[64,4,1,512]{3,1,2,0:T(4,128)}, u32[]{:S(2)}, u32[]{:S(2)}) %all-to-all-start.10) | async-done | bytes 524320 | tf_op jit(solution)/shard_map/all_to_all | solution.py:49
  494.8 100.0 %all-reduce = (f32[2,128]{1,0:T(2,128)}, f32[2,128,4]{1,2,0:T(4,128)}, f32[2,128]{1,0:T(2,128)}, f32[2,128]{1,0:T(2,128)}) all-reduce(f32[2,128]{1,0:T(2,128)S(1)} %pad_maximum_fusion.3, f32[2,128,4]{1,2,0:T(4,128)S(1)} %pad_maximum_fusion.2, ...), channel_id=1, replica_groups=mesh['row'=64,'head_0'=4,'head_1'=2] {'row','head_0','head_1'}, use_global_device_ids=true, to_apply=%region_31.32 | all-reduce | flops 1792 | bytes 14336 | tf_op jit(solution)/shard_map/psum | solution.py:355
  595.8 345.8 %all-reduce.4.cloned.1.call-done = (f32[2,4,128,128]{3,2,1,0:T(8,128)}, f32[2,128,128]{2,1,0:T(8,128)}) async-done(((f32[2,4,128,128]{3,2,1,0:T(8,128)}, f32[2,128,128]{2,1,0:T(8,128)}), (f32[2,4,128,128]{3,2,1,0:T(8,128)}, f32[2,128,128]{2,1,0:T(8,128)})) %all-reduce.4.cloned.1.call-update) | async-done | bytes 655376 | tf_op jit(solution)/shard_map/psum | solution.py:355
  941.6 1.9 copy.317
  (366 shorter events, 130.0 us)
Async XLA Ops:
  7.2 32.2 %copy-start.40 = (bf16[2,4,128,128]{3,2,1,0:T(8,128)(2,1)S(1)}, bf16[2,4,128,128]{3,2,1,0:T(8,128)(2,1)}, u32[]{:S(2)}) copy-start(bf16[2,4,128,128]{3,2,1,0:T(8,128)(2,1)} %param.22) | copy-start | bytes 786436
  7.2 33.1 %copy-start.68 = (f32[2,128]{1,0:T(2,128)S(1)}, f32[2,128]{1,0:T(2,128)}, u32[]{:S(2)}) copy-start(f32[2,128]{1,0:T(2,128)} %param.23) | copy-start | bytes 3076
  7.2 33.6 %copy-start.66 = (s32[512]{0:T(512)S(1)}, s32[512]{0:T(512)}, u32[]{:S(2)}) copy-start(s32[512]{0:T(512)} %param.19) | copy-start | bytes 6148
  7.2 55.9 %all-gather.3.cloned.1.call-start = ((), (), s32[]{:S(2)}) async-start(), calls=%async_computation.11 | async-start | bytes 1310720 | tf_op jit(solution)/shard_map/all_gather | solution.py:16
  9.5 30.8 %copy-start.53 = (f32[512]{0:T(512)}, f32[512]{0:T(512)S(1)}, u32[]{:S(2)}) copy-start(f32[512]{0:T(512)S(1)} %add_rsqrt_fusion.1) | copy-start | bytes 6148
  10.7 6.4 copy-start.57
  10.7 118.4 %copy-start.59 = (f32[128]{0:T(128)}, f32[128]{0:T(128)S(1)}, u32[]{:S(2)}) copy-start(f32[128]{0:T(128)S(1)} %get-tuple-element.487) | copy-start | bytes 1540
  11.9 53.3 %copy-start.18 = (bf16[1,512,128]{2,1,0:T(8,128)(2,1)}, bf16[1,512,128]{2,1,0:T(8,128)(2,1)S(1)}, u32[]{:S(2)}) copy-start(bf16[1,512,128]{2,1,0:T(8,128)(2,1)S(1)} %fusion.128) | copy-start | bytes 393220
  18.7 44.3 %all-to-all-start = ((bf16[64,4,1,512]{3,1,2,0:T(4,128)(2,1)}), bf16[64,4,1,512]{3,1,2,0:T(4,128)(2,1)S(1)}, u32[]{:S(2)}, u32[]{:S(2)}) async-start(bf16[64,4,1,512]{3,1,2,0:T(4,128)(2,1)} %broadcast_in_dim.57), calls=%async_computation | async-start | bytes 524288 | tf_op jit(solution)/shard_map/all_to_all | solution.py:28
  39.3 136.8 %all-gather.5.cloned.1.call-start = ((), (), s32[]{:S(2)}) async-start(), calls=%async_computation.12 | async-start | bytes 1310720 | tf_op jit(solution)/shard_map/all_gather | solution.py:16
  40.1 25.8 %copy-start.41 = (bf16[1,1,128,128]{2,3,1,0:T(8,128)(2,1)}, bf16[1,1,128,128]{2,3,1,0:T(8,128)(2,1)S(1)}, u32[]{:S(2)}) copy-start(bf16[1,1,128,128]{2,3,1,0:T(8,128)(2,1)S(1)} %copy.210) | copy-start | bytes 98308
  40.2 25.7 %copy-start.42 = (bf16[1,1,128,128]{2,3,1,0:T(8,128)(2,1)}, bf16[1,1,128,128]{2,3,1,0:T(8,128)(2,1)S(1)}, u32[]{:S(2)}) copy-start(bf16[1,1,128,128]{2,3,1,0:T(8,128)(2,1)S(1)} %copy.211) | copy-start | bytes 98308
  64.7 14.6 %copy-start.15 = (bf16[8,64,1,1,128]{4,1,0,3,2:T(8,128)(2,1)}, bf16[8,64,1,1,128]{4,1,0,3,2:T(8,128)(2,1)S(1)}, u32[]{:S(2)}) copy-start(bf16[8,64,1,1,128]{4,1,0,3,2:T(8,128)(2,1)S(1)} %copy.245) | copy-start | bytes 393220
  79.1 11.5 %copy-start.8 = (bf16[4,64,512]{2,1,0:T(8,128)(2,1)}, bf16[4,64,512]{2,1,0:T(8,128)(2,1)S(1)}, u32[]{:S(2)}) copy-start(bf16[4,64,512]{2,1,0:T(8,128)(2,1)S(1)} %get-tuple-element.911) | copy-start | bytes 786436
  79.1 11.4 %copy-start = (bf16[1,512,128]{2,1,0:T(8,128)(2,1)S(1)}, bf16[1,512,128]{2,1,0:T(8,128)(2,1)}, u32[]{:S(2)}) copy-start(bf16[1,512,128]{2,1,0:T(8,128)(2,1)} %param.17) | copy-start | bytes 393220
  79.1 11.5 %copy-start.28 = (bf16[1,512,128]{2,1,0:T(8,128)(2,1)S(1)}, bf16[1,512,128]{2,1,0:T(8,128)(2,1)}, u32[]{:S(2)}) copy-start(bf16[1,512,128]{2,1,0:T(8,128)(2,1)} %param.18) | copy-start | bytes 393220
  79.4 12.8 %copy-start.31 = (f32[8,64,128]{2,1,0:T(8,128)}, f32[8,64,128]{2,1,0:T(8,128)S(1)}, u32[]{:S(2)}) copy-start(f32[8,64,128]{2,1,0:T(8,128)S(1)} %copy.148) | copy-start | bytes 786436
  80.3 48.3 %copy-start.37 = (bf16[8,64,128]{2,1,0:T(8,128)(2,1)}, bf16[8,64,128]{2,1,0:T(8,128)(2,1)S(1)}, u32[]{:S(2)}) copy-start(bf16[8,64,128]{2,1,0:T(8,128)(2,1)S(1)} %get-tuple-element.481) | copy-start | bytes 393220
  90.7 38.4 %copy-start.65 = (f32[128]{0:T(128)S(1)}, f32[128]{0:T(128)}, u32[]{:S(2)}) copy-start(f32[128]{0:T(128)} %get-tuple-element.479) | copy-start | bytes 1540
  92.2 47.3 %copy-start.61 = (bf16[2,128,4]{1,2,0:T(4,128)(2,1)S(1)}, bf16[2,128,4]{1,2,0:T(4,128)(2,1)}, u32[]{:S(2)}) copy-start(bf16[2,128,4]{1,2,0:T(4,128)(2,1)} %param.25) | copy-start | bytes 6148
  128.5 23.1 %copy-start.52 = (bf16[1,1,128,128]{3,2,1,0:T(8,128)(2,1)S(1)}, bf16[1,1,128,128]{3,2,1,0:T(8,128)(2,1)}, u32[]{:S(2)}) copy-start(bf16[1,1,128,128]{3,2,1,0:T(8,128)(2,1)} %get-tuple-element.471) | copy-start | bytes 98308
  128.5 23.2 %copy-start.51 = (bf16[1,1,128,128]{3,2,1,0:T(8,128)(2,1)S(1)}, bf16[1,1,128,128]{3,2,1,0:T(8,128)(2,1)}, u32[]{:S(2)}) copy-start(bf16[1,1,128,128]{3,2,1,0:T(8,128)(2,1)} %get-tuple-element.474) | copy-start | bytes 98308
  128.7 23.2 %copy-start.49 = (bf16[2,128,128]{2,1,0:T(8,128)(2,1)S(1)}, bf16[2,128,128]{2,1,0:T(8,128)(2,1)}, u32[]{:S(2)}) copy-start(bf16[2,128,128]{2,1,0:T(8,128)(2,1)} %param.24) | copy-start | bytes 196612
  128.7 49.3 %copy-start.6 = (bf16[512,1,1,1,1,1,1,256]{7,0,5,4,3,2,1,6:T(8,128)(2,1)}, bf16[512,1,1,1,1,1,1,256]{7,0,5,4,3,2,1,6:T(8,128)(2,1)S(1)}, u32[]{:S(2)}) copy-start(bf16[512,1,1,1,1,1,1,256]{7,0,5,4,3,2,1,6:T(8,128)(2,1)S(1)} %copy.243) | copy-start | bytes 786436
  129.1 6.2 copy-start.55
  129.4 48.7 %copy-start.20 = (bf16[1,512,128]{2,1,0:T(8,128)(2,1)}, bf16[1,512,128]{2,1,0:T(8,128)(2,1)S(1)}, u32[]{:S(2)}) copy-start(bf16[1,512,128]{2,1,0:T(8,128)(2,1)S(1)} %fusion.136) | copy-start | bytes 393220
  136.1 8.6 all-to-all-start.4
  144.7 33.4 %copy-start.25 = (bf16[1,64,8,1,128]{4,1,3,0,2:T(8,128)(2,1)}, bf16[1,64,8,1,128]{4,1,3,0,2:T(8,128)(2,1)S(1)}, u32[]{:S(2)}) copy-start(bf16[1,64,8,1,128]{4,1,3,0,2:T(8,128)(2,1)S(1)} %all-to-all-done.4) | copy-start | bytes 393220
  145.4 29.9 %all-to-all-start.3 = ((bf16[64,4,1,512]{3,1,2,0:T(4,128)(2,1)}), bf16[64,4,1,512]{3,1,2,0:T(4,128)(2,1)S(1)}, u32[]{:S(2)}, u32[]{:S(2)}) async-start(bf16[64,4,1,512]{3,1,2,0:T(4,128)(2,1)} %broadcast_in_dim.74), calls=%async_computation.3 | async-start | bytes 524288 | tf_op jit(solution)/shard_map/all_to_all | solution.py:28
  151.7 26.3 %copy-start.44 = (bf16[1,1,128,128]{2,3,1,0:T(8,128)(2,1)}, bf16[1,1,128,128]{2,3,1,0:T(8,128)(2,1)S(1)}, u32[]{:S(2)}) copy-start(bf16[1,1,128,128]{2,3,1,0:T(8,128)(2,1)S(1)} %copy.213) | copy-start | bytes 98308
  151.9 26.4 %copy-start.46 = (bf16[1,1,128,128]{2,3,1,0:T(8,128)(2,1)}, bf16[1,1,128,128]{2,3,1,0:T(8,128)(2,1)S(1)}, u32[]{:S(2)}) copy-start(bf16[1,1,128,128]{2,3,1,0:T(8,128)(2,1)S(1)} %copy.214) | copy-start | bytes 98308
  181.5 19.6 %copy-start.17 = (bf16[8,64,1,1,128]{4,1,0,3,2:T(8,128)(2,1)}, bf16[8,64,1,1,128]{4,1,0,3,2:T(8,128)(2,1)S(1)}, u32[]{:S(2)}) copy-start(bf16[8,64,1,1,128]{4,1,0,3,2:T(8,128)(2,1)S(1)} %copy.244) | copy-start | bytes 393220
  182.5 18.6 %copy-start.70 = (f32[128]{0:T(128)S(1)}, f32[128]{0:T(128)}, u32[]{:S(2)}) copy-start(f32[128]{0:T(128)} %get-tuple-element.475) | copy-start | bytes 1540
  201.1 5.5 copy-start.33
  207.3 51.8 %copy-start.45 = (bf16[1,1,128,128]{2,3,1,0:T(8,128)(2,1)S(1)}, bf16[1,1,128,128]{2,3,1,0:T(8,128)(2,1)}, u32[]{:S(2)}) copy-start(bf16[1,1,128,128]{2,3,1,0:T(8,128)(2,1)} %copy-done.44) | copy-start | bytes 98308
  270.8 56.3 %copy-start.7 = (bf16[512,1,1,1,1,1,1,256]{7,0,5,4,3,2,1,6:T(8,128)(2,1)S(1)}, bf16[512,1,1,1,1,1,1,256]{7,0,5,4,3,2,1,6:T(8,128)(2,1)}, u32[]{:S(2)}) copy-start(bf16[512,1,1,1,1,1,1,256]{7,0,5,4,3,2,1,6:T(8,128)(2,1)} %copy-done.6) | copy-start | bytes 786436
  270.8 56.3 %copy-start.56 = (f32[512]{0:T(512)S(1)}, f32[512]{0:T(512)}, u32[]{:S(2)}) copy-start(f32[512]{0:T(512)} %copy-done.55) | copy-start | bytes 6148
  270.8 56.3 %copy-start.60 = (f32[128]{0:T(128)S(1)}, f32[128]{0:T(128)}, u32[]{:S(2)}) copy-start(f32[128]{0:T(128)} %copy-done.59) | copy-start | bytes 1540
  270.9 56.3 %copy-start.62 = (bf16[2,128,4]{1,2,0:T(4,128)(2,1)S(1)}, bf16[2,128,4]{1,2,0:T(4,128)(2,1)}, u32[]{:S(2)}) copy-start(bf16[2,128,4]{1,2,0:T(4,128)(2,1)} %param.25) | copy-start | bytes 6148
  288.8 38.1 %all-to-all-start.6 = ((f32[64,4,1,512]{3,1,2,0:T(4,128)}), f32[64,4,1,512]{3,1,2,0:T(4,128)S(1)}, u32[]{:S(2)}, u32[]{:S(2)}) async-start(f32[64,4,1,512]{3,1,2,0:T(4,128)} %bitcast.128), calls=%async_computation.6 | async-start | bytes 1048576 | tf_op jit(solution)/shard_map/all_to_all | solution.py:49
  293.5 73.0 %copy-start.29 = (bf16[1,512,128]{2,1,0:T(8,128)(2,1)S(1)}, bf16[1,512,128]{2,1,0:T(8,128)(2,1)}, u32[]{:S(2)}) copy-start(bf16[1,512,128]{2,1,0:T(8,128)(2,1)} %param.18) | copy-start | bytes 393220
  327.1 43.5 %copy-start.3 = (bf16[4,8,512,32]{2,3,1,0:T(8,128)(2,1)S(1)}, bf16[4,8,512,32]{2,3,1,0:T(8,128)(2,1)}, u32[]{:S(2)}) copy-start(bf16[4,8,512,32]{2,3,1,0:T(8,128)(2,1)} %get-tuple-element.225) | copy-start | bytes 3145732
  331.6 33.9 %all-to-all-start.7 = ((bf16[512,1,1,1,1,1,1,128]{7,6,5,4,3,2,1,0:T(2,128)(2,1)}), bf16[512,1,1,1,1,1,1,128]{7,6,5,4,3,2,1,0:T(2,128)(2,1)S(1)}, u32[]{:S(2)}, u32[]{:S(2)}) async-start(bf16[512,1,1,1,1,1,1,128]{7,6,5,4,3,2,1,0:T(2,128)(2,1)} %copy.171), calls=%async_computation.7 | async-start | bytes 524288 | tf_op jit(solution)/shard_map/all_to_all | solution.py:59
  340.8 35.0 %copy-start.32 = (f32[8,64,128]{2,1,0:T(8,128)S(1)}, f32[8,64,128]{2,1,0:T(8,128)}, u32[]{:S(2)}) copy-start(f32[8,64,128]{2,1,0:T(8,128)} %copy-done.31) | copy-start | bytes 786436
  340.8 35.0 %copy-start.50 = (bf16[2,128,128]{2,1,0:T(8,128)(2,1)S(1)}, bf16[2,128,128]{2,1,0:T(8,128)(2,1)}, u32[]{:S(2)}) copy-start(bf16[2,128,128]{2,1,0:T(8,128)(2,1)} %param.24) | copy-start | bytes 196612
  367.2 8.6 all-to-all-start.8
  375.8 5.3 copy-start.23
  377.0 48.6 %copy-start.26 = (bf16[8,64,128]{2,1,0:T(8,128)(2,1)}, bf16[8,64,128]{2,1,0:T(8,128)(2,1)S(1)}, u32[]{:S(2)}) copy-start(bf16[8,64,128]{2,1,0:T(8,128)(2,1)S(1)} %get-tuple-element.450) | copy-start | bytes 393220
  434.5 9.5 copy-start.10
  434.5 18.3 %all-to-all-start.9 = ((bf16[8,1,512,128]{3,2,1,0:T(8,128)(2,1)}), bf16[8,1,512,128]{3,2,1,0:T(8,128)(2,1)S(1)}, u32[]{:S(2)}, u32[]{:S(2)}) async-start(bf16[8,1,512,128]{3,2,1,0:T(8,128)(2,1)} %convert_bitcast_fusion), calls=%async_computation.9 | async-start | bytes 2097152 | tf_op jit(solution)/shard_map/all_to_all | solution.py:43
  440.5 20.9 %copy-start.1 = (bf16[4,8,512,32]{2,3,1,0:T(8,128)(2,1)S(1)}, bf16[4,8,512,32]{2,3,1,0:T(8,128)(2,1)}, u32[]{:S(2)}) copy-start(bf16[4,8,512,32]{2,3,1,0:T(8,128)(2,1)} %get-tuple-element.231) | copy-start | bytes 3145732
  445.8 15.4 %copy-start.21 = (bf16[1,512,128]{2,1,0:T(8,128)(2,1)S(1)}, bf16[1,512,128]{2,1,0:T(8,128)(2,1)}, u32[]{:S(2)}) copy-start(bf16[1,512,128]{2,1,0:T(8,128)(2,1)} %copy-done.20) | copy-start | bytes 393220
  452.8 40.0 %all-to-all-start.10 = ((f32[64,4,1,512]{3,1,2,0:T(4,128)}), f32[64,4,1,512]{3,1,2,0:T(4,128)}, u32[]{:S(2)}, u32[]{:S(2)}) async-start(f32[64,4,1,512]{3,1,2,0:T(4,128)} %bitcast.624), calls=%async_computation.10 | async-start | bytes 1048576 | tf_op jit(solution)/shard_map/all_to_all | solution.py:49
  459.5 482.1 %all-reduce.4.cloned.1.call-start = ((), (), s32[]{:S(2)}) async-start(), calls=%async_computation.13 | async-start | bytes 1310720 | tf_op jit(solution)/shard_map/psum | solution.py:355
  461.3 5.8 copy-start.24
  461.4 5.8 copy-start.38
  468.6 25.4 %copy-start.19 = (bf16[1,512,128]{2,1,0:T(8,128)(2,1)S(1)}, bf16[1,512,128]{2,1,0:T(8,128)(2,1)}, u32[]{:S(2)}) copy-start(bf16[1,512,128]{2,1,0:T(8,128)(2,1)} %copy-done.18) | copy-start | bytes 393220
  468.6 25.6 %copy-start.54 = (f32[512]{0:T(512)S(1)}, f32[512]{0:T(512)}, u32[]{:S(2)}) copy-start(f32[512]{0:T(512)} %copy-done.53) | copy-start | bytes 6148
  468.6 25.6 %copy-start.58 = (f32[128]{0:T(128)S(1)}, f32[128]{0:T(128)}, u32[]{:S(2)}) copy-start(f32[128]{0:T(128)} %copy-done.57) | copy-start | bytes 1540
  468.6 25.5 %copy-start.63 = (bf16[2,128,4]{1,2,0:T(4,128)(2,1)S(1)}, bf16[2,128,4]{1,2,0:T(4,128)(2,1)}, u32[]{:S(2)}) copy-start(bf16[2,128,4]{1,2,0:T(4,128)(2,1)} %param.25) | copy-start | bytes 6148
  469.5 25.2 %copy-start.64 = (f32[128]{0:T(128)S(1)}, f32[128]{0:T(128)}, u32[]{:S(2)}) copy-start(f32[128]{0:T(128)} %get-tuple-element.361) | copy-start | bytes 1540
  469.6 25.2 %copy-start.67 = (f32[128]{0:T(128)S(1)}, f32[128]{0:T(128)}, u32[]{:S(2)}) copy-start(f32[128]{0:T(128)} %get-tuple-element.355) | copy-start | bytes 1540
  469.6 125.2 %copy-start.14 = (f32[512,1,1,1,1,1,1,128]{7,6,5,4,3,2,1,0:T(1,128)S(1)}, f32[512,1,1,1,1,1,1,128]{7,6,5,4,3,2,1,0:T(1,128)}, u32[]{:S(2)}) copy-start(f32[512,1,1,1,1,1,1,128]{7,6,5,4,3,2,1,0:T(1,128)} %copy-done.13) | copy-start | bytes 786436
  469.6 125.2 %copy-start.30 = (bf16[1,512,128]{2,1,0:T(8,128)(2,1)S(1)}, bf16[1,512,128]{2,1,0:T(8,128)(2,1)}, u32[]{:S(2)}) copy-start(bf16[1,512,128]{2,1,0:T(8,128)(2,1)} %param.18) | copy-start | bytes 393220
  (18 other events, 47.6 us)
Sparse Core Ops, SparseCore 0:
  17.2 35.9 all-gather.2
  135.5 18.4 all-gather.4
  470.6 471.0 all-reduce.3
where the time goes:
time: 957 us; the launch traced here: 952 us
  waiting for transfers between devices  484 us (51%)
  blocking collectives  175 us (18%)
  matrix products  101 us (11%)
  local copies, waits for them, and re-layouts  82.8 us (9%)
  starting transfers between devices  57.9 us (6%)
  other arithmetic  35.6 us (4%)
  between operations  15 us (2%)
    psum x1, waiting for transfers between devices, local(): lax.psum((combined[0], combined[1], combined[2], combined[3], combined[4]...  346 us
    psum x1, blocking collectives, local(): lax.psum((combined[0], combined[1], combined[2], combined[3], combined[4]...  100 us
    all_to_all x2, waiting for transfers between devices, summed_on_arrival(): lax.all_to_all(parts, axis, split_axis=0, concat_axis=0, tiled=True)  54.8 us
    all_to_all x2, waiting for transfers between devices, from_everyone(): lax.all_to_all(jnp.broadcast_to(x[None], (length, *x.shape)), axis, 0, 0,...  45.5 us
    all_to_all x1, blocking collectives, joined_exchange(): parts = lax.all_to_all(parts, axis, split_axis=0, concat_axis=0, tiled=True)  36.4 us
    dynamic_update_slice x16, local copies, waits for them, and re-layouts, backward_block(): lax.map(differentiate, (log_totals, head_queries, head_pairs[0], head_pai...  30.2 us
    all_to_all x2, starting transfers between devices, from_everyone(): lax.all_to_all(jnp.broadcast_to(x[None], (length, *x.shape)), axis, 0, 0,...  26.7 us
    all_to_all x1, waiting for transfers between devices, joined_exchange(): parts = lax.all_to_all(parts, axis, split_axis=0, concat_axis=0, tiled=True)  24.7 us
  transfers between devices with their start and end apart: 11, of which 9 were waited for; matrix products, arithmetic and copies ran while one was open for 3% of the time, Pallas kernels for 0%

commit v1 on v0

--- a/solution.py
+++ b/solution.py
@@ -353,7 +353,11 @@
         for start_part, end_part in zip(first_weights, second_weights)
     ]
     stacked = lax.psum(
-        (combined[0], combined[1], combined[2], combined[3], combined[4], combined[5]), ROW_HEAD
+        lax.psum(
+            (combined[0], combined[1], combined[2], combined[3], combined[4], combined[5]),
+            ("head_0", "head_1"),
+        ),
+        "row",
     )
     return (pair_grad, stacked[0], stacked[1], stacked[2], stacked[3], stacked[4], stacked[5])
 

time: 957 us -> 1070 us (1.12)
  blocking collectives: 175 us -> 230 us
  waiting for transfers between devices: 484 us -> 537 us
    psum x0 -> x1, waiting for transfers between devices: none -> 344 us  [local(): lax.psum(lax.psum((combined[0], combined[1], combined[2], combined[3], co...]
    psum x1, waiting for transfers between devices: 346 us -> 84.5 us  [local(): lax.psum((combined[0], combined[1], combined[2], combined[3], combined[4]...]
    psum x0 -> x1, blocking collectives: none -> 142 us  [local(): lax.psum(lax.psum((combined[0], combined[1], combined[2], combined[3], co...]
    psum x1, blocking collectives: 100 us -> 13.4 us  [local(): lax.psum((combined[0], combined[1], combined[2], combined[3], combined[4]...]
    all_to_all x2, waiting for transfers between devices: 54.8 us -> 32.5 us  [summed_on_arrival(): lax.all_to_all(parts, axis, split_axis=0, concat_axis=0, tiled=True)]
  transfers between devices with their start and end apart: 11 -> 12, of which waited for: 9 -> 9; matrix products, arithmetic and copies ran while one was open for 3% -> 3% of each run, Pallas kernels for 0% -> 0%
where the time goes in v1:
time: 1070 us
  waiting for transfers between devices  537 us (50%)
  blocking collectives  230 us (21%)
  matrix products  102 us (10%)
  local copies, waits for them, and re-layouts  83.2 us (8%)
  starting transfers between devices  61 us (6%)
  other arithmetic  36.9 us (3%)
  between operations  15 us (1%)
    psum x1, waiting for transfers between devices, local(): lax.psum(lax.psum((combined[0], combined[1], combined[2], combined[3], co...  344 us
    psum x1, blocking collectives, local(): lax.psum(lax.psum((combined[0], combined[1], combined[2], combined[3], co...  142 us
    psum x1, waiting for transfers between devices, local(): lax.psum((combined[0], combined[1], combined[2], combined[3], combined[4]...  84.5 us
    all_to_all x2, waiting for transfers between devices, from_everyone(): lax.all_to_all(jnp.broadcast_to(x[None], (length, *x.shape)), axis, 0, 0,...  45.5 us
    all_to_all x1, blocking collectives, joined_exchange(): parts = lax.all_to_all(parts, axis, split_axis=0, concat_axis=0, tiled=True)  36.4 us
    all_to_all x2, waiting for transfers between devices, summed_on_arrival(): lax.all_to_all(parts, axis, split_axis=0, concat_axis=0, tiled=True)  32.5 us
    dynamic_update_slice x16, local copies, waits for them, and re-layouts, backward_block(): lax.map(differentiate, (log_totals, head_queries, head_pairs[0], head_pai...  30.2 us
    all_to_all x2, starting transfers between devices, from_everyone(): lax.all_to_all(jnp.broadcast_to(x[None], (length, *x.shape)), axis, 0, 0,...  26.7 us
  transfers between devices with their start and end apart: 12, of which 9 were waited for; matrix products, arithmetic and copies ran while one was open for 3% of the time, Pallas kernels for 0%

profile of v1, /device:TPU:1, one launch (start us, length us, event | category | flops | bytes accessed | tf_op | source)
XLA Modules:
  0.0 1065.5 jit_solution(5062274587073686059)
XLA Ops:
  12.4 5.2 all_gather.12
  19.2 20.5 %all-to-all-start = ((bf16[64,4,1,512]{3,1,2,0:T(4,128)(2,1)}), bf16[64,4,1,512]{3,1,2,0:T(4,128)(2,1)S(1)}, u32[]{:S(2)}, u32[]{:S(2)}) async-start(bf16[64,4,1,512]{3,1,2,0:T(4,128)(2,1)} %broadcast_in_dim.57), calls=%async_computation | async-start | bytes 524288 | tf_op jit(solution)/shard_map/all_to_all | solution.py:28
  41.3 22.2 %all-to-all-done = bf16[64,4,1,512]{3,1,2,0:T(4,128)(2,1)S(1)} async-done(((bf16[64,4,1,512]{3,1,2,0:T(4,128)(2,1)}), bf16[64,4,1,512]{3,1,2,0:T(4,128)(2,1)S(1)}, u32[]{:S(2)}, u32[]{:S(2)}) %all-to-all-start) | async-done | bytes 262176 | tf_op jit(solution)/shard_map/all_to_all | solution.py:28
  63.6 1.6 constant_dynamic-slice_fusion.3
  67.9 8.9 while.56
  79.5 9.2 all_to_all.79
  90.4 36.4 %all_to_all.80 = bf16[512,2,128]{2,1,0:T(2,128)(2,1)S(1)} all-to-all(bf16[512,2,128]{2,1,0:T(2,128)(2,1)S(1)} %reshape.464), channel_id=1, replica_groups=mesh['row'=64,'head_0'=4,'head_1'=2] {'row','head_0','head_1'}, dimensions={0} | all-to-all | bytes 524288 | tf_op jit(solution)/shard_map/all_to_all | solution.py:59
  127.6 6.0 all_gather.14
  134.3 3.4 all-to-all-start.4
  137.9 5.0 all-to-all-done.4
  143.7 6.2 all-to-all-start.3
  150.3 23.3 %all-to-all-done.3 = bf16[64,4,1,512]{3,1,2,0:T(4,128)(2,1)S(1)} async-done(((bf16[64,4,1,512]{3,1,2,0:T(4,128)(2,1)}), bf16[64,4,1,512]{3,1,2,0:T(4,128)(2,1)S(1)}, u32[]{:S(2)}, u32[]{:S(2)}) %all-to-all-start.3) | async-done | bytes 262176 | tf_op jit(solution)/shard_map/all_to_all | solution.py:28
  174.4 1.9 convolution_convert_fusion.4
  176.6 1.6 slice_bitcast_fusion
  180.8 18.3 %while.57 = (s32[]{:T(128)}, f32[4,8,64]{2,1,0:T(8,128)}, f32[4,8,64,32]{2,3,1,0:T(8,128)S(1)}, bf16[4,8,64,32]{2,3,1,0:T(8,128)(2,1)S(1)}, bf16[4,8,512,32]{2,3...) while((s32[]{:T(128)}, f32[4,8,64]{2,1,0:T(8,128)}, ...), condition=%wide.region_11.12_spmd, body=%wide.region_8.11_spmd.sunk | while | flops 35683840 | bytes 4221537 | solution.py:138
  205.5 51.8 %while.58 = (s32[]{:T(128)}, bf16[4,8,64,32]{2,3,1,0:T(8,128)(2,1)}, bf16[4,8,512,32]{2,3,1,0:T(8,128)(2,1)}, bf16[4,8,512,32]{2,3,1,0:T(8,128)(2,1)}, f32[4,64,...) while((s32[]{:T(128)}, ...), condition=%wide.region_15.16_spmd, body=%wide.region_12.15_spmd.sunk | while | flops 86801920 | bytes 10505361 | solution.py:217
  211.2 3.6 dynamic_update_slice.78
  214.9 1.8 fusion.300
  216.6 1.8 fusion.298
  224.2 3.6 dynamic_update_slice.78
  227.8 1.8 fusion.300
  229.6 1.8 fusion.298
  237.2 3.6 dynamic_update_slice.78
  240.8 1.8 fusion.300
  242.6 1.8 fusion.298
  250.1 3.6 dynamic_update_slice.78
  253.8 1.8 fusion.300
  255.5 1.8 fusion.298
  257.4 1.8 fusion.204
  261.2 1.7 fusion.100
  262.8 6.1 dynamic_update_slice.47
  269.1 17.9 %all_to_all.81 = bf16[8,1,512,128]{3,2,1,0:T(8,128)(2,1)S(1)} all-to-all(bf16[8,1,512,128]{3,2,1,0:T(8,128)(2,1)S(1)} %convert_bitcast_fusion.1), channel_id=1, replica_groups=mesh['row'=64,'head_0'=4,'head_1'=2] {'head_0','head_1'}, dimensions={0} | all-to-all | bytes 2097152 | tf_op jit(solution)/shard_map/all_to_all | solution.py:43
  287.0 5.5 all-to-all-start.6
  293.3 32.5 %all-to-all-done.6 = f32[64,4,1,512]{3,1,2,0:T(4,128)} async-done(((f32[64,4,1,512]{3,1,2,0:T(4,128)}), f32[64,4,1,512]{3,1,2,0:T(4,128)}, u32[]{:S(2)}, u32[]{:S(2)}) %all-to-all-start.6) | async-done | bytes 524320 | tf_op jit(solution)/shard_map/all_to_all | solution.py:49
  327.0 1.9 fusion.141
  332.4 11.3 %all-to-all-start.7 = ((bf16[512,1,1,1,1,1,1,128]{7,6,5,4,3,2,1,0:T(2,128)(2,1)}), bf16[512,1,1,1,1,1,1,128]{7,6,5,4,3,2,1,0:T(2,128)(2,1)}, u32[]{:S(2)}, u32[]{:S(2)}) async-start(bf16[512,1,1,1,1,1,1,128]{7,6,5,4,3,2,1,0:T(2,128)(2,1)} %copy.171), calls=%async_computation.7 | async-start | bytes 524288 | tf_op jit(solution)/shard_map/all_to_all | solution.py:59
  343.8 2.4 fusion.109
  346.1 20.1 %all-to-all-done.7 = bf16[512,1,1,1,1,1,1,128]{7,6,5,4,3,2,1,0:T(2,128)(2,1)} async-done(((bf16[512,1,1,1,1,1,1,128]{7,6,5,4,3,2,1,0:T(2,128)(2,1)}), bf16[512,1,1,1,1,1,1,128]{7,6,5,4,3,2,1,0:T(2,128)(2,1)}, u32[]{:S(2)}, u32[]{:S(2)}) %all-to-all-start.7) | async-done | bytes 131104 | tf_op jit(solution)/shard_map/all_to_all | solution.py:59
  369.2 3.4 all-to-all-start.8
  372.6 2.3 fusion.107
  374.8 2.9 all-to-all-done.8
  383.3 40.7 %while.59 = (s32[]{:T(128)}, bf16[4,8,64,32]{2,3,1,0:T(8,128)(2,1)}, bf16[4,8,512,32]{2,3,1,0:T(8,128)(2,1)}, bf16[4,8,512,32]{2,3,1,0:T(8,128)(2,1)}, f32[4,64,...) while((s32[]{:T(128)}, ...), condition=%wide.region_23.24_spmd, body=%wide.region_20.23_spmd.sunk | while | flops 86801920 | bytes 10505361 | solution.py:217
  388.0 3.6 dynamic_update_slice.82
  398.1 3.6 dynamic_update_slice.82
  408.3 3.6 dynamic_update_slice.82
  418.5 3.6 dynamic_update_slice.82
  424.0 1.8 fusion.205
  427.8 1.7 fusion.101
  429.4 6.1 dynamic_update_slice.48
  436.7 3.7 all-to-all-start.9
  440.4 1.8 convolution_bitcast_fusion.4
  443.7 1.6 copy.188
  446.5 1.6 maximum_bitcast_fusion.2
  448.1 1.9 convolution_bitcast_fusion.2
  450.0 1.6 fusion.113
  452.4 2.4 all-to-all-done.9
  454.8 6.9 all-to-all-start.10
  461.8 2.3 fusion.111
  469.3 84.5 %all-reduce.9.cloned.1.call-done = (f32[2,4,128,128]{3,2,1,0:T(8,128)}, f32[2,128,128]{2,1,0:T(8,128)}) async-done(((f32[2,4,128,128]{3,2,1,0:T(8,128)}, f32[2,128,128]{2,1,0:T(8,128)}), (f32[2,4,128,128]{3,2,1,0:T(8,128)}, f32[2,128,128]{2,1,0:T(8,128)})) %all-reduce.9.cloned.1.call-update) | async-done | bytes 655376 | tf_op jit(solution)/shard_map/psum | solution.py:356
  554.9 13.4 %all-reduce.2 = (f32[2,128]{1,0:T(2,128)S(1)}, f32[2,128,4]{1,2,0:T(4,128)S(1)}, f32[2,128]{1,0:T(2,128)S(1)}, f32[2,128]{1,0:T(2,128)S(1)}) all-reduce(f32[2,128]{1,0:T(2,128)S(1)} %pad_maximum_fusion.3, f32[2,128,4]{1,2,0:T(4,128)S(1)} %pad_maximum_fusion.2, ...), channel_id=1, replica_groups=mesh['row'=64,'head_0'=4,'head_1'=2] {'head_0','head_1'}, use_global_device_ids=true, to_apply=%region_32.33 | all-reduce | flops 1792 | bytes 14336 | tf_op jit(solution)/shard_map/psum | solution.py:356
  568.3 141.9 %all-reduce = (f32[2,128]{1,0:T(2,128)}, f32[2,128,4]{1,2,0:T(4,128)}, f32[2,128]{1,0:T(2,128)}, f32[2,128]{1,0:T(2,128)}) all-reduce(f32[2,128]{1,0:T(2,128)S(1)} %get-tuple-element.449, f32[2,128,4]{1,2,0:T(4,128)S(1)} %get-tuple-element.450, ...), channel_id=1, replica_groups=mesh['row'=64,'head_0'=4,'head_1'=2] {'row'}, use_global_device_ids=true, to_apply=%region_33.34 | all-reduce | flops 1792 | bytes 14336 | tf_op jit(solution)/shard_map/psum | solution.py:355
  711.3 344.3 %all-reduce.7.cloned.1.call-done = (f32[2,4,128,128]{3,2,1,0:T(8,128)}, f32[2,128,128]{2,1,0:T(8,128)}) async-done(((f32[2,4,128,128]{3,2,1,0:T(8,128)}, f32[2,128,128]{2,1,0:T(8,128)}), (f32[2,4,128,128]{3,2,1,0:T(8,128)}, f32[2,128,128]{2,1,0:T(8,128)})) %all-reduce.7.cloned.1.call-update) | async-done | bytes 655376 | tf_op jit(solution)/shard_map/psum | solution.py:355
  1055.6 1.9 copy.319
  1057.4 1.6 copy.320
  (362 shorter events, 133.5 us)
Async XLA Ops:
  7.2 32.7 %copy-start.38 = (bf16[2,4,128,128]{3,2,1,0:T(8,128)(2,1)S(1)}, bf16[2,4,128,128]{3,2,1,0:T(8,128)(2,1)}, u32[]{:S(2)}) copy-start(bf16[2,4,128,128]{3,2,1,0:T(8,128)(2,1)} %param.22) | copy-start | bytes 786436
  7.2 33.6 %copy-start.64 = (f32[2,128]{1,0:T(2,128)S(1)}, f32[2,128]{1,0:T(2,128)}, u32[]{:S(2)}) copy-start(f32[2,128]{1,0:T(2,128)} %param.23) | copy-start | bytes 3076
  7.2 34.1 %copy-start.62 = (s32[512]{0:T(512)S(1)}, s32[512]{0:T(512)}, u32[]{:S(2)}) copy-start(s32[512]{0:T(512)} %param.19) | copy-start | bytes 6148
  7.2 56.4 %all-gather.3.cloned.1.call-start = ((), (), s32[]{:S(2)}) async-start(), calls=%async_computation.11 | async-start | bytes 1310720 | tf_op jit(solution)/shard_map/all_gather | solution.py:16
  9.5 31.3 %copy-start.51 = (f32[512]{0:T(512)}, f32[512]{0:T(512)S(1)}, u32[]{:S(2)}) copy-start(f32[512]{0:T(512)S(1)} %add_rsqrt_fusion.1) | copy-start | bytes 6148
  10.7 116.6 %copy-start.56 = (f32[128]{0:T(128)}, f32[128]{0:T(128)S(1)}, u32[]{:S(2)}) copy-start(f32[128]{0:T(128)S(1)} %get-tuple-element.493) | copy-start | bytes 1540
  12.4 53.3 %copy-start.17 = (bf16[1,512,128]{2,1,0:T(8,128)(2,1)}, bf16[1,512,128]{2,1,0:T(8,128)(2,1)S(1)}, u32[]{:S(2)}) copy-start(bf16[1,512,128]{2,1,0:T(8,128)(2,1)S(1)} %fusion.128) | copy-start | bytes 393220
  19.2 44.3 %all-to-all-start = ((bf16[64,4,1,512]{3,1,2,0:T(4,128)(2,1)}), bf16[64,4,1,512]{3,1,2,0:T(4,128)(2,1)S(1)}, u32[]{:S(2)}, u32[]{:S(2)}) async-start(bf16[64,4,1,512]{3,1,2,0:T(4,128)(2,1)} %broadcast_in_dim.57), calls=%async_computation | async-start | bytes 524288 | tf_op jit(solution)/shard_map/all_to_all | solution.py:28
  39.8 134.6 %all-gather.5.cloned.1.call-start = ((), (), s32[]{:S(2)}) async-start(), calls=%async_computation.12 | async-start | bytes 1310720 | tf_op jit(solution)/shard_map/all_gather | solution.py:16
  40.6 25.8 %copy-start.39 = (bf16[1,1,128,128]{2,3,1,0:T(8,128)(2,1)}, bf16[1,1,128,128]{2,3,1,0:T(8,128)(2,1)S(1)}, u32[]{:S(2)}) copy-start(bf16[1,1,128,128]{2,3,1,0:T(8,128)(2,1)S(1)} %copy.210) | copy-start | bytes 98308
  40.7 25.7 %copy-start.40 = (bf16[1,1,128,128]{2,3,1,0:T(8,128)(2,1)}, bf16[1,1,128,128]{2,3,1,0:T(8,128)(2,1)S(1)}, u32[]{:S(2)}) copy-start(bf16[1,1,128,128]{2,3,1,0:T(8,128)(2,1)S(1)} %copy.211) | copy-start | bytes 98308
  65.2 12.4 %copy-start.14 = (bf16[8,64,1,1,128]{4,1,0,3,2:T(8,128)(2,1)}, bf16[8,64,1,1,128]{4,1,0,3,2:T(8,128)(2,1)S(1)}, u32[]{:S(2)}) copy-start(bf16[8,64,1,1,128]{4,1,0,3,2:T(8,128)(2,1)S(1)} %copy.245) | copy-start | bytes 393220
  76.8 12.1 %copy-start.7 = (bf16[4,64,512]{2,1,0:T(8,128)(2,1)}, bf16[4,64,512]{2,1,0:T(8,128)(2,1)S(1)}, u32[]{:S(2)}) copy-start(bf16[4,64,512]{2,1,0:T(8,128)(2,1)S(1)} %get-tuple-element.921) | copy-start | bytes 786436
  76.8 11.9 %copy-start = (bf16[1,512,128]{2,1,0:T(8,128)(2,1)S(1)}, bf16[1,512,128]{2,1,0:T(8,128)(2,1)}, u32[]{:S(2)}) copy-start(bf16[1,512,128]{2,1,0:T(8,128)(2,1)} %param.17) | copy-start | bytes 393220
  77.4 11.5 %copy-start.27 = (bf16[1,512,128]{2,1,0:T(8,128)(2,1)S(1)}, bf16[1,512,128]{2,1,0:T(8,128)(2,1)}, u32[]{:S(2)}) copy-start(bf16[1,512,128]{2,1,0:T(8,128)(2,1)} %param.18) | copy-start | bytes 393220
  77.6 12.8 %copy-start.29 = (f32[8,64,128]{2,1,0:T(8,128)}, f32[8,64,128]{2,1,0:T(8,128)S(1)}, u32[]{:S(2)}) copy-start(f32[8,64,128]{2,1,0:T(8,128)S(1)} %copy.148) | copy-start | bytes 786436
  78.6 48.3 %copy-start.35 = (bf16[8,64,128]{2,1,0:T(8,128)(2,1)}, bf16[8,64,128]{2,1,0:T(8,128)(2,1)S(1)}, u32[]{:S(2)}) copy-start(bf16[8,64,128]{2,1,0:T(8,128)(2,1)S(1)} %get-tuple-element.487) | copy-start | bytes 393220
  88.9 38.5 %copy-start.61 = (f32[128]{0:T(128)S(1)}, f32[128]{0:T(128)}, u32[]{:S(2)}) copy-start(f32[128]{0:T(128)} %get-tuple-element.485) | copy-start | bytes 1540
  90.4 47.3 %copy-start.57 = (bf16[2,128,4]{1,2,0:T(4,128)(2,1)S(1)}, bf16[2,128,4]{1,2,0:T(4,128)(2,1)}, u32[]{:S(2)}) copy-start(bf16[2,128,4]{1,2,0:T(4,128)(2,1)} %param.25) | copy-start | bytes 6148
  126.8 23.1 %copy-start.49 = (bf16[1,1,128,128]{3,2,1,0:T(8,128)(2,1)S(1)}, bf16[1,1,128,128]{3,2,1,0:T(8,128)(2,1)}, u32[]{:S(2)}) copy-start(bf16[1,1,128,128]{3,2,1,0:T(8,128)(2,1)} %get-tuple-element.477) | copy-start | bytes 98308
  126.8 23.2 %copy-start.48 = (bf16[1,1,128,128]{3,2,1,0:T(8,128)(2,1)S(1)}, bf16[1,1,128,128]{3,2,1,0:T(8,128)(2,1)}, u32[]{:S(2)}) copy-start(bf16[1,1,128,128]{3,2,1,0:T(8,128)(2,1)} %get-tuple-element.480) | copy-start | bytes 98308
  126.9 23.2 %copy-start.47 = (bf16[2,128,128]{2,1,0:T(8,128)(2,1)S(1)}, bf16[2,128,128]{2,1,0:T(8,128)(2,1)}, u32[]{:S(2)}) copy-start(bf16[2,128,128]{2,1,0:T(8,128)(2,1)} %param.24) | copy-start | bytes 196612
  127.0 49.3 %copy-start.6 = (bf16[512,1,1,1,1,1,1,256]{7,0,5,4,3,2,1,6:T(8,128)(2,1)}, bf16[512,1,1,1,1,1,1,256]{7,0,5,4,3,2,1,6:T(8,128)(2,1)S(1)}, u32[]{:S(2)}) copy-start(bf16[512,1,1,1,1,1,1,256]{7,0,5,4,3,2,1,6:T(8,128)(2,1)S(1)} %copy.243) | copy-start | bytes 786436
  127.4 6.2 copy-start.53
  127.6 48.7 %copy-start.19 = (bf16[1,512,128]{2,1,0:T(8,128)(2,1)}, bf16[1,512,128]{2,1,0:T(8,128)(2,1)S(1)}, u32[]{:S(2)}) copy-start(bf16[1,512,128]{2,1,0:T(8,128)(2,1)S(1)} %fusion.136) | copy-start | bytes 393220
  134.3 8.6 all-to-all-start.4
  142.9 33.4 %copy-start.24 = (bf16[1,64,8,1,128]{4,1,3,0,2:T(8,128)(2,1)}, bf16[1,64,8,1,128]{4,1,3,0,2:T(8,128)(2,1)S(1)}, u32[]{:S(2)}) copy-start(bf16[1,64,8,1,128]{4,1,3,0,2:T(8,128)(2,1)S(1)} %all-to-all-done.4) | copy-start | bytes 393220
  143.7 29.9 %all-to-all-start.3 = ((bf16[64,4,1,512]{3,1,2,0:T(4,128)(2,1)}), bf16[64,4,1,512]{3,1,2,0:T(4,128)(2,1)S(1)}, u32[]{:S(2)}, u32[]{:S(2)}) async-start(bf16[64,4,1,512]{3,1,2,0:T(4,128)(2,1)} %broadcast_in_dim.74), calls=%async_computation.3 | async-start | bytes 524288 | tf_op jit(solution)/shard_map/all_to_all | solution.py:28
  150.0 26.3 %copy-start.42 = (bf16[1,1,128,128]{2,3,1,0:T(8,128)(2,1)}, bf16[1,1,128,128]{2,3,1,0:T(8,128)(2,1)S(1)}, u32[]{:S(2)}) copy-start(bf16[1,1,128,128]{2,3,1,0:T(8,128)(2,1)S(1)} %copy.213) | copy-start | bytes 98308
  150.1 26.4 %copy-start.44 = (bf16[1,1,128,128]{2,3,1,0:T(8,128)(2,1)}, bf16[1,1,128,128]{2,3,1,0:T(8,128)(2,1)S(1)}, u32[]{:S(2)}) copy-start(bf16[1,1,128,128]{2,3,1,0:T(8,128)(2,1)S(1)} %copy.214) | copy-start | bytes 98308
  179.7 19.6 %copy-start.16 = (bf16[8,64,1,1,128]{4,1,0,3,2:T(8,128)(2,1)}, bf16[8,64,1,1,128]{4,1,0,3,2:T(8,128)(2,1)S(1)}, u32[]{:S(2)}) copy-start(bf16[8,64,1,1,128]{4,1,0,3,2:T(8,128)(2,1)S(1)} %copy.244) | copy-start | bytes 393220
  180.8 18.6 %copy-start.66 = (f32[128]{0:T(128)S(1)}, f32[128]{0:T(128)}, u32[]{:S(2)}) copy-start(f32[128]{0:T(128)} %get-tuple-element.481) | copy-start | bytes 1540
  199.3 5.5 copy-start.31
  205.5 51.8 %copy-start.43 = (bf16[1,1,128,128]{2,3,1,0:T(8,128)(2,1)S(1)}, bf16[1,1,128,128]{2,3,1,0:T(8,128)(2,1)}, u32[]{:S(2)}) copy-start(bf16[1,1,128,128]{2,3,1,0:T(8,128)(2,1)} %copy-done.42) | copy-start | bytes 98308
  287.0 38.8 %all-to-all-start.6 = ((f32[64,4,1,512]{3,1,2,0:T(4,128)}), f32[64,4,1,512]{3,1,2,0:T(4,128)}, u32[]{:S(2)}, u32[]{:S(2)}) async-start(f32[64,4,1,512]{3,1,2,0:T(4,128)} %bitcast.128), calls=%async_computation.6 | async-start | bytes 1048576 | tf_op jit(solution)/shard_map/all_to_all | solution.py:49
  292.5 51.3 %copy-start.3 = (bf16[4,8,512,32]{2,3,1,0:T(8,128)(2,1)S(1)}, bf16[4,8,512,32]{2,3,1,0:T(8,128)(2,1)}, u32[]{:S(2)}) copy-start(bf16[4,8,512,32]{2,3,1,0:T(8,128)(2,1)} %get-tuple-element.225) | copy-start | bytes 3145732
  332.4 33.8 %all-to-all-start.7 = ((bf16[512,1,1,1,1,1,1,128]{7,6,5,4,3,2,1,0:T(2,128)(2,1)}), bf16[512,1,1,1,1,1,1,128]{7,6,5,4,3,2,1,0:T(2,128)(2,1)}, u32[]{:S(2)}, u32[]{:S(2)}) async-start(bf16[512,1,1,1,1,1,1,128]{7,6,5,4,3,2,1,0:T(2,128)(2,1)} %copy.171), calls=%async_computation.7 | async-start | bytes 524288 | tf_op jit(solution)/shard_map/all_to_all | solution.py:59
  343.7 28.8 %copy-start.5 = (bf16[4,8,512,32]{2,3,1,0:T(8,128)(2,1)S(1)}, bf16[4,8,512,32]{2,3,1,0:T(8,128)(2,1)}, u32[]{:S(2)}) copy-start(bf16[4,8,512,32]{2,3,1,0:T(8,128)(2,1)} %get-tuple-element.226) | copy-start | bytes 3145732
  346.1 31.6 %copy-start.30 = (f32[8,64,128]{2,1,0:T(8,128)S(1)}, f32[8,64,128]{2,1,0:T(8,128)}, u32[]{:S(2)}) copy-start(f32[8,64,128]{2,1,0:T(8,128)} %copy-done.29) | copy-start | bytes 786436
  346.1 31.6 %copy-start.46 = (f32[8,64,128]{2,1,0:T(8,128)S(1)}, f32[8,64,128]{2,1,0:T(8,128)}, u32[]{:S(2)}) copy-start(f32[8,64,128]{2,1,0:T(8,128)} %get-tuple-element.488) | copy-start | bytes 786436
  367.4 11.8 %copy-start.12 = (f32[512,1,1,1,1,1,1,128]{7,6,5,4,3,2,1,0:T(1,128)}, f32[512,1,1,1,1,1,1,128]{7,6,5,4,3,2,1,0:T(1,128)S(1)}, u32[]{:S(2)}) copy-start(f32[512,1,1,1,1,1,1,128]{7,6,5,4,3,2,1,0:T(1,128)S(1)} %convert_element_type.274) | copy-start | bytes 786436
  369.2 8.6 all-to-all-start.8
  377.7 5.5 copy-start.22
  379.3 48.5 %copy-start.25 = (bf16[8,64,128]{2,1,0:T(8,128)(2,1)}, bf16[8,64,128]{2,1,0:T(8,128)(2,1)S(1)}, u32[]{:S(2)}) copy-start(bf16[8,64,128]{2,1,0:T(8,128)(2,1)S(1)} %get-tuple-element.456) | copy-start | bytes 393220
  436.7 8.7 copy-start.9
  436.7 13.4 %copy-start.1 = (bf16[4,8,512,32]{2,3,1,0:T(8,128)(2,1)S(1)}, bf16[4,8,512,32]{2,3,1,0:T(8,128)(2,1)}, u32[]{:S(2)}) copy-start(bf16[4,8,512,32]{2,3,1,0:T(8,128)(2,1)} %get-tuple-element.231) | copy-start | bytes 3145732
  436.7 18.2 %all-to-all-start.9 = ((bf16[8,1,512,128]{3,2,1,0:T(8,128)(2,1)}), bf16[8,1,512,128]{3,2,1,0:T(8,128)(2,1)S(1)}, u32[]{:S(2)}, u32[]{:S(2)}) async-start(bf16[8,1,512,128]{3,2,1,0:T(8,128)(2,1)} %convert_bitcast_fusion), calls=%async_computation.9 | async-start | bytes 2097152 | tf_op jit(solution)/shard_map/all_to_all | solution.py:43
  451.7 13.4 %copy-start.23 = (bf16[1,64,8,1,128]{4,1,3,0,2:T(8,128)(2,1)S(1)}, bf16[1,64,8,1,128]{4,1,3,0,2:T(8,128)(2,1)}, u32[]{:S(2)}) copy-start(bf16[1,64,8,1,128]{4,1,3,0,2:T(8,128)(2,1)} %copy-done.22) | copy-start | bytes 393220
  451.7 13.4 %copy-start.36 = (bf16[8,64,128]{2,1,0:T(8,128)(2,1)S(1)}, bf16[8,64,128]{2,1,0:T(8,128)(2,1)}, u32[]{:S(2)}) copy-start(bf16[8,64,128]{2,1,0:T(8,128)(2,1)} %copy-done.35) | copy-start | bytes 393220
  454.8 12.0 %copy-start.15 = (bf16[8,64,1,1,128]{4,1,0,3,2:T(8,128)(2,1)S(1)}, bf16[8,64,1,1,128]{4,1,0,3,2:T(8,128)(2,1)}, u32[]{:S(2)}) copy-start(bf16[8,64,1,1,128]{4,1,0,3,2:T(8,128)(2,1)} %copy-done.14) | copy-start | bytes 393220
  454.8 12.0 %copy-start.26 = (bf16[8,64,128]{2,1,0:T(8,128)(2,1)S(1)}, bf16[8,64,128]{2,1,0:T(8,128)(2,1)}, u32[]{:S(2)}) copy-start(bf16[8,64,128]{2,1,0:T(8,128)(2,1)} %copy-done.25) | copy-start | bytes 393220
  454.8 12.2 %copy-start.11 = (bf16[8,64,4,32]{1,3,2,0:T(8,128)(2,1)S(1)}, bf16[8,64,4,32]{1,3,2,0:T(8,128)(2,1)}, u32[]{:S(2)}) copy-start(bf16[8,64,4,32]{1,3,2,0:T(8,128)(2,1)} %copy-done.10) | copy-start | bytes 393220
  454.8 99.2 %all-to-all-start.10 = ((f32[64,4,1,512]{3,1,2,0:T(4,128)}), f32[64,4,1,512]{3,1,2,0:T(4,128)S(1)}, u32[]{:S(2)}, u32[]{:S(2)}) async-start(f32[64,4,1,512]{3,1,2,0:T(4,128)} %bitcast.624), calls=%async_computation.10 | async-start | bytes 1048576 | tf_op jit(solution)/shard_map/all_to_all | solution.py:49
  461.7 92.1 %all-reduce.9.cloned.1.call-start = ((), (), s32[]{:S(2)}) async-start(), calls=%async_computation.14 | async-start | bytes 1310720 | tf_op jit(solution)/shard_map/psum | solution.py:356
  464.1 5.3 copy-start.65
  468.2 86.0 %copy-start.18 = (bf16[1,512,128]{2,1,0:T(8,128)(2,1)S(1)}, bf16[1,512,128]{2,1,0:T(8,128)(2,1)}, u32[]{:S(2)}) copy-start(bf16[1,512,128]{2,1,0:T(8,128)(2,1)} %copy-done.17) | copy-start | bytes 393220
  468.2 86.1 %copy-start.52 = (f32[512]{0:T(512)S(1)}, f32[512]{0:T(512)}, u32[]{:S(2)}) copy-start(f32[512]{0:T(512)} %copy-done.51) | copy-start | bytes 6148
  468.2 86.1 %copy-start.55 = (f32[128]{0:T(128)S(1)}, f32[128]{0:T(128)}, u32[]{:S(2)}) copy-start(f32[128]{0:T(128)} %copy-done.54) | copy-start | bytes 1540
  468.2 86.1 %copy-start.58 = (bf16[2,128,4]{1,2,0:T(4,128)(2,1)S(1)}, bf16[2,128,4]{1,2,0:T(4,128)(2,1)}, u32[]{:S(2)}) copy-start(bf16[2,128,4]{1,2,0:T(4,128)(2,1)} %param.25) | copy-start | bytes 6148
  469.1 85.8 %copy-start.60 = (f32[128]{0:T(128)S(1)}, f32[128]{0:T(128)}, u32[]{:S(2)}) copy-start(f32[128]{0:T(128)} %get-tuple-element.361) | copy-start | bytes 1540
  469.1 85.8 %copy-start.63 = (f32[128]{0:T(128)S(1)}, f32[128]{0:T(128)}, u32[]{:S(2)}) copy-start(f32[128]{0:T(128)} %get-tuple-element.355) | copy-start | bytes 1540
  469.1 241.1 %copy-start.13 = (f32[512,1,1,1,1,1,1,128]{7,6,5,4,3,2,1,0:T(1,128)S(1)}, f32[512,1,1,1,1,1,1,128]{7,6,5,4,3,2,1,0:T(1,128)}, u32[]{:S(2)}) copy-start(f32[512,1,1,1,1,1,1,128]{7,6,5,4,3,2,1,0:T(1,128)} %copy-done.12) | copy-start | bytes 786436
  469.1 241.1 %copy-start.28 = (bf16[1,512,128]{2,1,0:T(8,128)(2,1)S(1)}, bf16[1,512,128]{2,1,0:T(8,128)(2,1)}, u32[]{:S(2)}) copy-start(bf16[1,512,128]{2,1,0:T(8,128)(2,1)} %param.18) | copy-start | bytes 393220
  469.1 586.4 %all-reduce.7.cloned.1.call-start = ((), (), s32[]{:S(2)}) async-start(), calls=%async_computation.13 | async-start | bytes 1310720 | tf_op jit(solution)/shard_map/psum | solution.py:355
  (15 other events, 34.1 us)
Sparse Core Ops, SparseCore 0:
  17.7 35.9 all-gather.2
  133.8 18.4 all-gather.4
  469.2 84.5 all-reduce.8
  556.7 498.8 all-reduce.6
